TPU v7x, 32 devices: a 4x4x1 block of a 4x4x8 slice. The times are simulated.
32 devices in a mesh: dp: 1 (over z), tp: 32 (over x, y, core).
Axes of the slice: x: 4, y: 4, z: 1, core: 2. Of those that a mesh axis runs over, the one named last changes fastest.
The devices are a block of a 4x4x8 slice.
Arguments:
- x: bfloat16 [8192, 4096], P(('dp', 'tp'))
- w_gate: bfloat16 [4096, 16384], P(None, 'tp')
- w_up: bfloat16 [4096, 16384], P(None, 'tp')
- w_down: bfloat16 [16384, 4096], P('tp')
Outputs:
- output: bfloat16 [8192, 4096], P(('dp', 'tp'))
All inputs are finite; a program needn't handle non-finite values.
Results may differ from a plain program's by a relative error of at most 0.016.
Values are sent between devices in bfloat16 or wider.
A program may use at most 768 MiB of HBM per device.

v0:
```python
import jax
import jax.numpy as jnp
from jax import lax
from jax.sharding import PartitionSpec as P


def solution(mesh):
    def step(x, w_gate, w_up, w_down):
        rows = lax.all_gather(x, "tp", axis=0, tiled=True)
        gate = jnp.dot(rows, w_gate, preferred_element_type=jnp.float32)
        up = jnp.dot(rows, w_up, preferred_element_type=jnp.float32)
        hidden = (jax.nn.silu(gate) * up).astype(jnp.bfloat16)
        term = jnp.dot(hidden, w_down, preferred_element_type=jnp.float32).astype(jnp.bfloat16)
        return lax.psum_scatter(term, "tp", scatter_dimension=0, tiled=True)

    return jax.shard_map(
        step,
        mesh=mesh,
        in_specs=(P(("dp", "tp"), None), P(None, "tp"), P(None, "tp"), P("tp", None)),
        out_specs=P(("dp", "tp"), None),
        check_vma=False,
    )
```

profile of v0, /device:TPU:97, one launch (start us, length us, event | category | flops | bytes accessed | tf_op | source)
XLA Modules:
  0.0 623.4 jit_solution(18117332719966417181)
XLA Ops:
  6.5 0.0 all-gather.2.cloned.1.call-start
  6.6 0.7 all-gather.2.cloned.1.call-update
  7.3 0.1 reduce-scatter.4.cloned.1.call-start
  7.4 202.2 %all-gather.2.cloned.1.call-done = bf16[8192,4096]{1,0:T(8,128)(2,1)} async-done(((bf16[256,4096]{1,0:T(8,128)(2,1)}), bf16[8192,4096]{1,0:T(8,128)(2,1)}) %all-gather.2.cloned.1.call-update) | async-done | bytes 67108880 | tf_op jit(solution)/shard_map/all_gather | solution.py:9
  209.6 42.9 %fusion = f32[8192,512]{1,0:T(8,128)} fusion(bf16[8192,4096]{1,0:T(8,128)(2,1)} %all-gather.2.cloned.1.call-done, bf16[4096,512]{1,0:T(8,128)(2,1)} %param.5), kind=kOutput, calls=%fused_computation.2 | convolution fusion | flops 34359738368 | bytes 88080384 | tf_op jit(solution)/shard_map/dot_general | solution.py:10
  252.5 81.0 %convolution_convert_fusion = bf16[8192,4096]{1,0:T(8,128)(2,1)} fusion(bf16[512,4096]{1,0:T(8,128)(2,1)} %param.7, f32[8192,512]{1,0:T(8,128)} %fusion, bf16[8192,4096]{1,0:T(8,128)(2,1)} %all-gather.2.cloned.1.call-done, bf16[4096,512]{1,0:T(8,128)(2,1)} %param.6), kind=kOutput, calls=%fused_computation | convolution fusion | flops 68778196992 | bytes 159383552 | tf_op jit(solution)/shard_map/dot_general | solution.py:13
  333.4 0.1 reduce-scatter.4.cloned.1.call-update
  333.5 283.0 %reduce-scatter.4.cloned.1.call-done = bf16[256,4096]{1,0:T(8,128)(2,1)} async-done(((bf16[8192,4096]{1,0:T(8,128)(2,1)}), bf16[256,4096]{1,0:T(8,128)(2,1)}) %reduce-scatter.4.cloned.1.call-update) | async-done | bytes 2097168
Async XLA Ops:
  6.5 203.0 %all-gather.2.cloned.1.call-start = ((), (), s32[]{:S(2)}) async-start(), calls=%async_computation.1 | async-start | bytes 69206016 | tf_op jit(solution)/shard_map/all_gather | solution.py:9
  7.3 609.2 %reduce-scatter.4.cloned.1.call-start = ((), (), s32[]{:S(2)}) async-start(), calls=%async_computation.2 | async-start | bytes 69206016
Sparse Core Ops, SparseCore 0:
  9.4 200.1 all-gather.1
  333.6 282.8 reduce-scatter.3
where the time goes:
time: 623 us
  waiting for transfers between devices  486 us (78%)
  matrix products  124 us (20%)
  between operations  13.4 us (2%)
    unnamed x3, waiting for transfers between devices  284 us
    all_gather x1, waiting for transfers between devices, step(): rows = lax.all_gather(x, 'tp', axis=0, tiled=True)  202 us
    dot_general x1, matrix products, step(): jnp.dot(hidden, w_down, preferred_element_type=jnp.float32)  81 us
    dot_general x1, matrix products, step(): gate = jnp.dot(rows, w_gate, preferred_element_type=jnp.float32)  42.9 us
  transfers between devices with their start and end apart: 2, of which 2 were waited for; matrix products, arithmetic and copies ran while one was open for 0% of the time, Pallas kernels for 0%

commit v1 on v0

v1 whole, which is shorter than its diff:
```python
import functools
import math

import jax
import jax.numpy as jnp
from jax import lax
from jax.experimental import pallas as pl
from jax.experimental.pallas import tpu as pltpu
from jax.sharding import PartitionSpec as P

MESH = pl.DeviceIdType.MESH
NX, NP, NU, NB = 7, 5, 3, 2


def neighbours(side):
    me = lax.axis_index("tp")
    chip, core = me // 2, me % 2
    gx, gy = chip // side, chip % side
    diagonal = (gx + gy) % side
    ahead_x = ((diagonal + 1) // side + core) % 2
    behind_x = ((side - diagonal) // side + core) % 2
    after = ((gx + ahead_x) % side) * side + (gy + 1 - ahead_x) % side
    before = ((gx + side - behind_x) % side) * side + (gy + side - 1 + behind_x) % side
    return after * 2 + core, before * 2 + core, chip * 2 + 1 - core


def kernel(
    n, x_hbm, wg_hbm, wu_hbm, wd_hbm, y_hbm,
    tok, arr, out, sib, term, acc, hid, wg, wu, wd,
    x_sem, w_sem, y_sem, tok_send, tok_recv, swap_send, swap_recv,
    out_send, out_recv, term_send, term_recv,
):
    half = x_hbm.shape[0] // 2
    q = half // 2
    depth, width = x_hbm.shape[1], wg_hbm.shape[1]
    items = n
    after, before, sibling = neighbours(math.isqrt(n // 2))
    targets = (after, before)

    def x_load(i):
        return pltpu.make_async_copy(x_hbm.at[pl.ds(i * half, half)], tok.at[i, pl.ds(0, half)], x_sem.at[i])

    loads = [
        pltpu.make_async_copy(a, b, w_sem.at[k]) for k, (a, b) in enumerate(((wg_hbm, wg), (wu_hbm, wu), (wd_hbm, wd)))
    ]

    def y_store(i):
        return pltpu.make_async_copy(out.at[i], y_hbm.at[pl.ds(i * half, half)], y_sem.at[i])

    def tok_copy(i, r):
        here, there = i % NX, (i + 2) % NX
        return pltpu.make_async_remote_copy(
            src_ref=tok.at[here, pl.ds(r * q, q)],
            dst_ref=tok.at[there, pl.ds(r * q, q)],
            send_sem=tok_send.at[r, here],
            recv_sem=tok_recv.at[r, there],
            device_id={"tp": targets[r]},
            device_id_type=MESH,
        )

    def swap_copy(i):
        slot = i % NX
        return pltpu.make_async_remote_copy(
            src_ref=tok.at[slot, pl.ds(0, half)],
            dst_ref=tok.at[slot, pl.ds(half, half)],
            send_sem=swap_send.at[slot],
            recv_sem=swap_recv.at[slot],
            device_id={"tp": sibling},
            device_id_type=MESH,
        )

    def sib_slot(i):
        return jnp.where(i < 2, i, 2 + i % NU)

    def acc_slot(i):
        return jnp.where(i < 2, i, 2 + i % NB)

    def term_copy(i):
        here, there = i % NB, sib_slot(i)
        return pltpu.make_async_remote_copy(
            src_ref=term.at[here],
            dst_ref=sib.at[there],
            send_sem=term_send.at[here],
            recv_sem=term_recv.at[there],
            device_id={"tp": sibling},
            device_id_type=MESH,
        )

    def out_copy(i, r):
        here, there = i % NB, (i + 2) % NP
        return pltpu.make_async_remote_copy(
            src_ref=out.at[here, pl.ds(r * q, q)],
            dst_ref=arr.at[there, pl.ds(r * q, q)],
            send_sem=out_send.at[r, here],
            recv_sem=out_recv.at[r, there],
            device_id={"tp": targets[r]},
            device_id_type=MESH,
        )

    for i in range(2):
        x_load(i).start()
    for load in loads:
        load.start()
    barrier = pltpu.get_barrier_semaphore()
    for device in (after, before, sibling):
        pl.semaphore_signal(barrier, inc=1, device_id={"tp": device}, device_id_type=MESH)
    pl.semaphore_wait(barrier, 3)

    def compute(i):
        slot, here, mine = i % NX, i % NB, acc_slot(i)
        step = min(256, width)
        for c in range(0, width, step):
            rows = tok[slot]
            gate = jnp.dot(rows, wg[:, c : c + step], preferred_element_type=jnp.float32)
            up = jnp.dot(rows, wu[:, c : c + step], preferred_element_type=jnp.float32)
            hid[:, c : c + step] = (jax.nn.silu(gate) * up).astype(jnp.bfloat16)
        step = min(512, depth)
        for c in range(0, depth, step):
            t = jnp.dot(hid[...], wd[:, c : c + step], preferred_element_type=jnp.float32)
            acc[mine, :, c : c + step] = t[:half]
            term[here, :, c : c + step] = t[half:].astype(jnp.bfloat16)

    def add(i, arrived):
        here, mine, theirs, slot = i % NB, i % items, i % items, i % NP
        mine, theirs = acc_slot(mine), sib_slot(theirs)
        step = min(512, depth)

        def piece(c, _):
            cols = pl.ds(pl.multiple_of(c * step, step), step)
            total = acc[mine, :, cols] + sib[theirs, :, cols].astype(jnp.float32)
            if arrived:
                total = total + arr[slot, :, cols].astype(jnp.float32)
            out[here, :, cols] = total.astype(jnp.bfloat16)
            return 0

        lax.fori_loop(0, depth // step, piece, 0)

    def tick(i, _):
        @pl.when(i < 2)
        def _():
            x_load(i).wait()

        @pl.when((i >= 2) & (i < items))
        def _():
            for r in range(2):
                tok_copy(i - 2, r).wait_recv()

        @pl.when(i < items - 2)
        def _():
            for r in range(2):
                tok_copy(i, r).start()

        @pl.when(i < items)
        def _():
            swap_copy(i).start()

        @pl.when((i >= 2) & (i < items))
        def _():
            for r in range(2):
                tok_copy(i - 2, r).wait_send()

        @pl.when((i >= 2) & (i < items + 2))
        def _():
            swap_copy(i - 2).wait_send()

        @pl.when(i == 1)
        def _():
            for load in loads:
                load.wait()

        k = i - 1

        @pl.when((k >= 0) & (k < items))
        def _():
            swap_copy(k).wait_recv()

        @pl.when((k >= 2) & (k < items + 2))
        def _():
            term_copy(k - 2).wait_send()

        @pl.when((k >= 0) & (k < items))
        def _():
            compute(k)
            term_copy(k).start()

        j = i - 2

        @pl.when(j >= 2)
        def _():
            term_copy(j % items).wait_recv()

        @pl.when(j >= 4)
        def _():
            for r in range(2):
                out_copy(j - 2, r).wait_recv()
            for r in range(2):
                out_copy(j - 2, r).wait_send()
            add(j, True)

        @pl.when((j >= 2) & (j < 4))
        def _():
            add(j, False)

        @pl.when((j >= 2) & (j < items))
        def _():
            for r in range(2):
                out_copy(j, r).start()

        @pl.when(j >= items)
        def _():
            y_store(j - items).start()

        return 0

    lax.fori_loop(0, items + 4, tick, 0)
    for i in range(2):
        y_store(i).wait()


def solution(mesh):
    n = mesh.shape["tp"]

    def step(x, w_gate, w_up, w_down):
        rows, depth = x.shape
        width = w_gate.shape[1]
        half = rows // 2
        vmem, dma = pltpu.VMEM, pltpu.SemaphoreType.DMA
        return pl.pallas_call(
            functools.partial(kernel, n),
            out_shape=jax.ShapeDtypeStruct((rows, depth), jnp.bfloat16),
            in_specs=[pl.BlockSpec(memory_space=pl.ANY)] * 4,
            out_specs=pl.BlockSpec(memory_space=pl.ANY),
            scratch_shapes=[
                vmem((NX, 2 * half, depth), jnp.bfloat16),
                vmem((NP, half, depth), jnp.bfloat16),
                vmem((NB, half, depth), jnp.bfloat16),
                vmem((2 + NU, half, depth), jnp.bfloat16),
                vmem((NB, half, depth), jnp.bfloat16),
                vmem((2 + NB, half, depth), jnp.float32),
                vmem((2 * half, width), jnp.bfloat16),
                vmem((depth, width), jnp.bfloat16),
                vmem((depth, width), jnp.bfloat16),
                vmem((width, depth), jnp.bfloat16),
                dma((2,)),
                dma((3,)),
                dma((2,)),
                dma((2, NX)),
                dma((2, NX)),
                dma((NX,)),
                dma((NX,)),
                dma((2, NB)),
                dma((2, NP)),
                dma((NB,)),
                dma((2 + NU,)),
            ],
            compiler_params=pltpu.CompilerParams(
                collective_id=0, has_side_effects=True, vmem_limit_bytes=63 * 1024 * 1024
            ),
        )(x, w_gate, w_up, w_down)

    return jax.shard_map(
        step,
        mesh=mesh,
        in_specs=(P(("dp", "tp"), None), P(None, "tp"), P(None, "tp"), P("tp", None)),
        out_specs=P(("dp", "tp"), None),
        check_vma=False,
    )
```

time: 623 us -> 352 us (0.57)
  waiting for transfers between devices: 486 us -> 0 us
  Pallas kernels: 0 us -> 348 us
  matrix products: 124 us -> 0 us
  between operations: 13.4 us -> 0.01 us
    pallas_call x0 -> x1, Pallas kernels: none -> 348 us  [step(): pl.pallas_call(functools.partial(kernel, n), out_shape=jax.ShapeDtypeStru...]
    unnamed x3 -> x0, waiting for transfers between devices: 284 us -> none
    all_gather x1 -> x0, waiting for transfers between devices: 202 us -> none  [step(): rows = lax.all_gather(x, 'tp', axis=0, tiled=True)]
    dot_general x2 -> x0, matrix products: 124 us -> none  [the longest x1 81 us: step(): jnp.dot(hidden, w_down, preferred_element_type=jnp.float32)]
  transfers between devices with their start and end apart: 2 -> 0, of which waited for: 2 -> 0; matrix products, arithmetic and copies ran while one was open for 0% -> 0% of each run, Pallas kernels for 0% -> 0%
where the time goes in v1:
time: 352 us
  Pallas kernels  348 us (99%)
    pallas_call x1, Pallas kernels, step(): pl.pallas_call(functools.partial(kernel, n), out_shape=jax.ShapeDtypeStru...  348 us

profile of v1, /device:TPU:97, one launch (start us, length us, event | category | flops | bytes accessed | tf_op | source)
XLA Modules:
  0.0 351.6 jit_solution(5782929748057381418)
XLA Ops:
  0.0 348.4 %shard_map.46 = bf16[256,4096]{1,0:T(8,128)(2,1)} custom-call(bf16[256,4096]{1,0:T(8,128)(2,1)} %x_hbm.1, bf16[4096,512]{1,0:T(8,128)(2,1)} %wg_hbm.1, bf16[4096,512]{1,0:T(8,128)(2,1)} %wu_hbm.1, bf16[512,4096]{1,0:T(8,128)(2,1)} %wd_hbm.1), custom_call_target="tpu_custom_call" | custom-call | tf_op jit(solution)/shard_map/pallas_call | solution.py:228
  348.5 3.1 copy.6

commit v2 on v0

v2 whole, which is shorter than its diff:
```python
import functools
import math

import jax
import jax.numpy as jnp
from jax import lax
from jax.experimental import pallas as pl
from jax.experimental.pallas import tpu as pltpu
from jax.sharding import PartitionSpec as P

MESH = pl.DeviceIdType.MESH
DOWN = (
    ("a", 0, None),
    ("e", 2, None),
    ("c", 1, "a"),
    ("f", 1, "e"),
    ("h", 1, "c"),
    ("g", 3, "e"),
    ("i", 0, "h"),
    ("b", 0, "a"),
    ("j", 2, "h"),
    ("d", 3, "a"),
)
HOP = {name: hop for name, hop, _ in DOWN}
TRANSIT = ("a", "e", "h")
UP = ("i", "j", "b", "h", "d", "c", "f", "g", "a", "e")
BELOW = {name: tuple(n for n, _, parent in DOWN if parent == name) for name in UP}
LANDED = {"c": 0, "f": 1, "g": 2, "i": 3, "b": 4, "j": 5, "d": 6}
ARRIVED = {"i": 0, "j": 1, "b": 2, "h": 3, "d": 4, "c": 5, "f": 6, "g": 0, "a": 1, "e": 7}
OWN = 7
HIDDEN = {"own": 0, "c": 1, "f": 2, "g": 3, "i": 4, "b": 5, "j": 6, "d": 7}
STEPS = len(DOWN)
LAG = 3
UP0 = 2 * STEPS
ROOT0 = UP0 + 2 * STEPS + 1
NS, NO, NV = 4, 3, 2


def table(index, values):
    result = values[0]
    for k, value in enumerate(values[1:], 1):
        result = jnp.where(index == k, value, result)
    return result


def kernel(
    n, x_hbm, wg_hbm, wu_hbm, wd_hbm, y_hbm, far,
    tok, swp, out, term, sib, acc, hid, wg, wu, wd,
    x_sem, w_sem, y_sem, w_send, w_recv, tok_send, tok_recv, swap_send, swap_recv,
    out_send, out_recv, term_send, term_recv,
):
    half = x_hbm.shape[0] // 2
    q = half // 2
    depth, width = x_hbm.shape[1], wg_hbm.shape[1]
    part = width // 2
    side = math.isqrt(n // 2)
    me = lax.axis_index("tp")
    chip, core = me // 2, me % 2
    gx, gy = chip // side, chip % side
    sibling = chip * 2 + 1 - core

    def neighbour(hop):
        turn = (hop + core) % 4
        dx = (1 - turn) * ((turn + 1) % 2)
        dy = (2 - turn) * (turn % 2)
        return (((gx + dx + side) % side) * side + (gy + dy + side) % side) * 2 + core

    around = [neighbour(hop) for hop in range(4)]

    def remote(src, dst, send, recv, device):
        return pltpu.make_async_remote_copy(
            src_ref=src, dst_ref=dst, send_sem=send, recv_sem=recv, device_id={"tp": device}, device_id_type=MESH
        )

    def rows(r):
        return pl.ds(r * q, q)

    def landing(name, h, r):
        if name in TRANSIT:
            return far.at[2 * TRANSIT.index(name) + h, rows(r)]
        return tok.at[2 * LANDED[name] + h, rows(r)]

    def tok_copy(t, h, r):
        name, hop, parent = DOWN[t]
        src = x_hbm.at[pl.ds(h * half + r * q, q)] if parent is None else landing(parent, h, r)
        return remote(
            src, landing(name, h, r), tok_send.at[r, 2 * t + h], tok_recv.at[r, 2 * t + h], around[(hop + 2 * r) % 4]
        )

    def swap_copy(k, h):
        item = 2 * k + h
        src = x_hbm.at[pl.ds(h * half, half)] if k == 0 else tok.at[2 * (k - 1) + h]
        return remote(src, swp.at[item % NS], swap_send.at[item % NS], swap_recv.at[item % NS], sibling)

    def out_copy(s, h, r):
        item = 2 * s + h
        name = UP[s]
        return remote(
            out.at[item % NO, rows(r)],
            tok.at[2 * ARRIVED[name] + h, rows(r)],
            out_send.at[r, item % NO],
            out_recv.at[r, item],
            around[(HOP[name] + 2 + 2 * r) % 4],
        )

    def term_copy(item):
        return remote(term.at[item % NV], sib.at[item % NV], term_send.at[item % NV], term_recv.at[item % NV], sibling)

    def root_copy(h):
        return remote(term.at[h], swp.at[h], term_send.at[h], swap_recv.at[h], sibling)

    def x_load(h):
        return pltpu.make_async_copy(x_hbm.at[pl.ds(h * half, half)], tok.at[2 * OWN + h], x_sem.at[h])

    def y_store(h):
        slot = (ROOT0 - UP0 + h) % NO
        return pltpu.make_async_copy(out.at[slot], y_hbm.at[pl.ds(h * half, half)], y_sem.at[h])

    loads = []
    gifts = []
    for r in range(2):
        cols = pl.ds(r * part, part)
        theirs = pl.ds(width + r * part, part)
        for k, (a, b) in enumerate(((wg_hbm, wg), (wu_hbm, wu))):
            loads.append(pltpu.make_async_copy(a.at[:, cols], b.at[r], w_sem.at[2 * k + r]))
            gifts.append(remote(a.at[:, cols], b.at[2 + r], w_send.at[r, k], w_recv.at[r, k], around[2 * r]))
        gifts.append(remote(wd_hbm.at[cols], wd.at[theirs], w_send.at[r, 2], w_recv.at[r, 2], around[2 * r]))
    loads.append(pltpu.make_async_copy(wd_hbm, wd.at[pl.ds(0, width)], w_sem.at[4]))

    barrier = pltpu.get_barrier_semaphore()
    for device in (*around, sibling):
        pl.semaphore_signal(barrier, inc=1, device_id={"tp": device}, device_id_type=MESH)
    pl.semaphore_wait(barrier, 5)
    for gift in gifts:
        gift.start()
    for h in range(2):
        x_load(h).start()
    for load in loads:
        load.start()

    def compute(k, h):
        mine = 2 * ((k + OWN) % 8) + h
        item = 2 * k + h
        theirs = item % NS
        for g in range(4):
            block = jnp.concatenate([tok[mine], swp[theirs]], axis=0)
            gate = jnp.dot(block, wg[g], preferred_element_type=jnp.float32)
            up = jnp.dot(block, wu[g], preferred_element_type=jnp.float32)
            hid[item, :, g * part : (g + 1) * part] = (jax.nn.silu(gate) * up).astype(jnp.bfloat16)

    def project(item, slot):
        step = min(512, depth)
        for c in range(0, depth, step):
            t = jnp.dot(hid[item], wd[:, c : c + step], preferred_element_type=jnp.float32)
            acc[:, c : c + step] = t[:half]
            term[slot, :, c : c + step] = t[half:].astype(jnp.bfloat16)

    def add(slot, terms, theirs, arrived, h):
        step = min(512, depth)

        def piece(c, _):
            cols = pl.ds(pl.multiple_of(c * step, step), step)
            parts = [acc[:, cols], theirs(cols).astype(jnp.float32)] if terms else []
            for name in arrived:
                parts.append(tok[2 * ARRIVED[name] + h, :, cols].astype(jnp.float32))
            total = parts[0]
            for p in parts[1:]:
                total = total + p
            out[slot, :, cols] = total.astype(jnp.bfloat16)
            return 0

        lax.fori_loop(0, depth // step, piece, 0)

    def during(i, first):
        return (i >= first) & (i < first + 2), i - first

    def tick(i, _):
        for t in range(STEPS):
            now, h = during(i, 2 * t + LAG)

            @pl.when(now)
            def _(t=t, h=h):
                for r in range(2):
                    tok_copy(t, h, r).wait_recv()

        for t in range(STEPS):
            now, h = during(i, 2 * t)

            @pl.when(now)
            def _(t=t, h=h):
                for r in range(2):
                    tok_copy(t, h, r).start()

            now, h = during(i, 2 * t + LAG + 1)

            @pl.when(now)
            def _(t=t, h=h):
                for r in range(2):
                    tok_copy(t, h, r).wait_send()

        for name, k in HIDDEN.items():
            first = 0 if k == 0 else 2 * [s for s, _, _ in DOWN].index(name) + LAG
            now, h = during(i, first + 2)

            @pl.when(now)
            def _(k=k, h=h):
                swap_copy(k, h).wait_send()

        for name, k in HIDDEN.items():
            first = 0 if k == 0 else 2 * [s for s, _, _ in DOWN].index(name) + LAG
            now, h = during(i, first)

            @pl.when(now)
            def _(k=k, h=h):
                swap_copy(k, h).start()

        for s, name in enumerate(UP):
            now, h = during(i, UP0 + 2 * s + LAG)

            @pl.when(now)
            def _(s=s, h=h):
                for r in range(2):
                    out_copy(s, h, r).wait_recv()
                for r in range(2):
                    out_copy(s, h, r).wait_send()

        for s, name in enumerate(UP):
            now, h = during(i, UP0 + 2 * s)

            @pl.when(now)
            def _(s=s, name=name, h=h):
                item = 2 * s + h
                terms = name not in TRANSIT
                if terms:
                    term_copy(item).wait_recv()
                    term_copy(item).wait_send()
                add(item % NO, terms, lambda cols: sib[item % NV, :, cols], BELOW[name], h)
                for r in range(2):
                    out_copy(s, h, r).start()

        now, h = during(i, ROOT0)

        @pl.when(now)
        def _(h=h):
            root_copy(h).wait_recv()
            root_copy(h).wait_send()
            add((ROOT0 - UP0 + h) % NO, True, lambda cols: swp[h, :, cols], ("a", "e"), h)
            y_store(h).start()

        @pl.when(i == 4)
        def _():
            for h in range(2):
                x_load(h).wait()
            for load in loads:
                load.wait()
            for gift in gifts:
                gift.wait_recv()

        pair = i // 2
        firsts = [2 if k == 0 else [s for s, _, _ in DOWN].index(name) + 2 for name, k in HIDDEN.items()]
        k = table(pair, [firsts.index(p) if p in firsts else -1 for p in range(max(firsts) + 1)] + [-1])
        k = jnp.where(pair <= max(firsts), k, -1)

        @pl.when(k >= 0)
        def _():
            for c in range(8):
                now, h = during(i, 2 * firsts[c])

                @pl.when(now)
                def _(c=c, h=h):
                    swap_copy(c, h).wait_recv()

            compute(k, i % 2)

        item = i + 1 - UP0
        kinds = [-1 if name in TRANSIT else HIDDEN[name] for name in UP]
        k = jnp.where((item >= 0) & (item < 2 * STEPS), table(item // 2, kinds), -1)
        last = i + 1 - ROOT0
        root = (last >= 0) & (last < 2)

        @pl.when((k >= 0) | root)
        def _():
            slot = jnp.where(root, last, item % NV)
            project(jnp.where(root, last, 2 * k + item % 2), slot)

            @pl.when(root)
            def _():
                root_copy(last).start()

            @pl.when(k >= 0)
            def _():
                term_copy(item).start()

        return 0

    lax.fori_loop(0, ROOT0 + 2, tick, 0)
    for gift in gifts:
        gift.wait_send()
    for h in range(2):
        y_store(h).wait()


def solution(mesh):
    n = mesh.shape["tp"]

    def step(x, w_gate, w_up, w_down):
        rows, depth = x.shape
        width = w_gate.shape[1]
        half, part = rows // 2, width // 2
        vmem, dma = pltpu.VMEM, pltpu.SemaphoreType.DMA
        y, _ = pl.pallas_call(
            functools.partial(kernel, n),
            out_shape=(
                jax.ShapeDtypeStruct((rows, depth), jnp.bfloat16),
                jax.ShapeDtypeStruct((2 * len(TRANSIT), half, depth), jnp.bfloat16),
            ),
            in_specs=[pl.BlockSpec(memory_space=pl.ANY)] * 4,
            out_specs=(pl.BlockSpec(memory_space=pl.ANY),) * 2,
            scratch_shapes=[
                vmem((16, half, depth), jnp.bfloat16),
                vmem((NS, half, depth), jnp.bfloat16),
                vmem((NO, half, depth), jnp.bfloat16),
                vmem((NV, half, depth), jnp.bfloat16),
                vmem((NV, half, depth), jnp.bfloat16),
                vmem((half, depth), jnp.float32),
                vmem((16, 2 * half, 2 * width), jnp.bfloat16),
                vmem((4, depth, part), jnp.bfloat16),
                vmem((4, depth, part), jnp.bfloat16),
                vmem((2 * width, depth), jnp.bfloat16),
                dma((2,)),
                dma((5,)),
                dma((2,)),
                dma((2, 3)),
                dma((2, 3)),
                dma((2, 2 * STEPS)),
                dma((2, 2 * STEPS)),
                dma((NS,)),
                dma((NS,)),
                dma((2, NO)),
                dma((2, 2 * STEPS)),
                dma((NV,)),
                dma((NV,)),
            ],
            compiler_params=pltpu.CompilerParams(
                collective_id=0, has_side_effects=True, vmem_limit_bytes=67_043_328
            ),
        )(x, w_gate, w_up, w_down)
        return y

    return jax.shard_map(
        step,
        mesh=mesh,
        in_specs=(P(("dp", "tp"), None), P(None, "tp"), P(None, "tp"), P("tp", None)),
        out_specs=P(("dp", "tp"), None),
        check_vma=False,
    )
```

time: 623 us -> 332 us (0.53)
  waiting for transfers between devices: 486 us -> 0 us
  Pallas kernels: 0 us -> 328 us
  matrix products: 124 us -> 0 us
  between operations: 13.4 us -> 0.01 us
    pallas_call x0 -> x1, Pallas kernels: none -> 328 us  [step(): pl.pallas_call(functools.partial(kernel, n), out_shape=(jax.ShapeDtypeStr...]
    unnamed x3 -> x0, waiting for transfers between devices: 284 us -> none
    all_gather x1 -> x0, waiting for transfers between devices: 202 us -> none  [step(): rows = lax.all_gather(x, 'tp', axis=0, tiled=True)]
    dot_general x2 -> x0, matrix products: 124 us -> none  [the longest x1 81 us: step(): jnp.dot(hidden, w_down, preferred_element_type=jnp.float32)]
  transfers between devices with their start and end apart: 2 -> 0, of which waited for: 2 -> 0; matrix products, arithmetic and copies ran while one was open for 0% -> 0% of each run, Pallas kernels for 0% -> 0%
where the time goes in v2:
time: 332 us
  Pallas kernels  328 us (99%)
    pallas_call x1, Pallas kernels, step(): pl.pallas_call(functools.partial(kernel, n), out_shape=(jax.ShapeDtypeStr...  328 us

profile of v2, /device:TPU:97, one launch (start us, length us, event | category | flops | bytes accessed | tf_op | source)
XLA Modules:
  0.0 331.6 jit_solution(11352821118688353151)
XLA Ops:
  0.0 328.4 %shard_map.46 = (bf16[256,4096]{1,0:T(8,128)(2,1)}, bf16[6,128,4096]{2,1,0:T(8,128)(2,1)}) custom-call(bf16[256,4096]{1,0:T(8,128)(2,1)} %x_hbm.1, bf16[4096,512]{1,0:T(8,128)(2,1)} %wg_hbm.1, bf16[4096,512]{1,0:T(8,128)(2,1)} %wu_hbm.1, bf16[512,4096]{1,0:T(8,128)(2,1)} %wd_hbm.1), custom_call_target="tpu_custom_call" | custom-call | tf_op jit(solution)/shard_map/pallas_call | solution.py:311
  328.5 3.1 copy.6

commit v3 on v2

--- a/solution.py
+++ b/solution.py
@@ -21,19 +21,19 @@
     ("j", 2, "h"),
     ("d", 3, "a"),
 )
-HOP = {name: hop for name, hop, _ in DOWN}
+TREE = {name: (hop, parent) for name, hop, parent in DOWN}
 TRANSIT = ("a", "e", "h")
-UP = ("i", "j", "b", "h", "d", "c", "f", "g", "a", "e")
-BELOW = {name: tuple(n for n, _, parent in DOWN if parent == name) for name in UP}
-LANDED = {"c": 0, "f": 1, "g": 2, "i": 3, "b": 4, "j": 5, "d": 6}
-ARRIVED = {"i": 0, "j": 1, "b": 2, "h": 3, "d": 4, "c": 5, "f": 6, "g": 0, "a": 1, "e": 7}
+ORDER = "aecfhgiFjGbIdJBHDCEA"
+AT = {name: 2 * place for place, name in enumerate(ORDER)}
+BELOW = {name.upper(): tuple(n.upper() for n, _, parent in DOWN if parent == name) for name, _, _ in DOWN}
+LANDED = {"c": 0, "f": 1, "g": 2, "i": 3, "j": 4, "b": 5, "d": 6}
+ARRIVED = {"F": 7, "G": 0, "I": 1, "J": 2, "B": 3, "H": 4, "D": 5, "C": 6, "E": 1, "A": 2}
 OWN = 7
-HIDDEN = {"own": 0, "c": 1, "f": 2, "g": 3, "i": 4, "b": 5, "j": 6, "d": 7}
-STEPS = len(DOWN)
-LAG = 3
-UP0 = 2 * STEPS
-ROOT0 = UP0 + 2 * STEPS + 1
-NS, NO, NV = 4, 3, 2
+HIDDEN = {"own": 0, "c": 1, "f": 2, "g": 3, "i": 4, "j": 5, "b": 6, "d": 7}
+TICKS = 2 * len(ORDER)
+LAG = 4
+ROOT0 = TICKS + LAG - 2
+NS, NO, NV = 4, 4, 2
 
 
 def table(index, values):
@@ -46,8 +46,7 @@
 def kernel(
     n, x_hbm, wg_hbm, wu_hbm, wd_hbm, y_hbm, far,
     tok, swp, out, term, sib, acc, hid, wg, wu, wd,
-    x_sem, w_sem, y_sem, w_send, w_recv, tok_send, tok_recv, swap_send, swap_recv,
-    out_send, out_recv, term_send, term_recv,
+    x_sem, w_sem, y_sem, w_send, w_recv, hop_send, hop_recv, swap_send, swap_recv, term_send, term_recv, free_sem,
 ):
     half = x_hbm.shape[0] // 2
     q = half // 2
@@ -80,11 +79,12 @@
             return far.at[2 * TRANSIT.index(name) + h, rows(r)]
         return tok.at[2 * LANDED[name] + h, rows(r)]
 
-    def tok_copy(t, h, r):
-        name, hop, parent = DOWN[t]
+    def tok_copy(name, h, r):
+        hop, parent = TREE[name]
+        item = AT[name] + h
         src = x_hbm.at[pl.ds(h * half + r * q, q)] if parent is None else landing(parent, h, r)
         return remote(
-            src, landing(name, h, r), tok_send.at[r, 2 * t + h], tok_recv.at[r, 2 * t + h], around[(hop + 2 * r) % 4]
+            src, landing(name, h, r), hop_send.at[r, item], hop_recv.at[r, item], around[(hop + 2 * r) % 4]
         )
 
     def swap_copy(k, h):
@@ -92,16 +92,18 @@
         src = x_hbm.at[pl.ds(h * half, half)] if k == 0 else tok.at[2 * (k - 1) + h]
         return remote(src, swp.at[item % NS], swap_send.at[item % NS], swap_recv.at[item % NS], sibling)
 
-    def out_copy(s, h, r):
-        item = 2 * s + h
-        name = UP[s]
+    def sum_copy(name, h, r):
+        item = AT[name] + h
         return remote(
             out.at[item % NO, rows(r)],
             tok.at[2 * ARRIVED[name] + h, rows(r)],
-            out_send.at[r, item % NO],
-            out_recv.at[r, item],
-            around[(HOP[name] + 2 + 2 * r) % 4],
+            hop_send.at[r, item],
+            hop_recv.at[r, item],
+            around[(TREE[name.lower()][0] + 2 + 2 * r) % 4],
         )
+
+    def hop_copy(name, h, r):
+        return tok_copy(name, h, r) if name in TREE else sum_copy(name, h, r)
 
     def term_copy(item):
         return remote(term.at[item % NV], sib.at[item % NV], term_send.at[item % NV], term_recv.at[item % NV], sibling)
@@ -113,7 +115,7 @@
         return pltpu.make_async_copy(x_hbm.at[pl.ds(h * half, half)], tok.at[2 * OWN + h], x_sem.at[h])
 
     def y_store(h):
-        slot = (ROOT0 - UP0 + h) % NO
+        slot = (ROOT0 + h) % NO
         return pltpu.make_async_copy(out.at[slot], y_hbm.at[pl.ds(h * half, half)], y_sem.at[h])
 
     loads = []
@@ -131,7 +133,7 @@
     for device in (*around, sibling):
         pl.semaphore_signal(barrier, inc=1, device_id={"tp": device}, device_id_type=MESH)
     pl.semaphore_wait(barrier, 5)
-    for gift in gifts:
+    for gift in gifts[:2] + gifts[3:5]:
         gift.start()
     for h in range(2):
         x_load(h).start()
@@ -174,69 +176,55 @@
     def during(i, first):
         return (i >= first) & (i < first + 2), i - first
 
+    swaps = [(0 if k == 0 else AT[name] + LAG, k) for name, k in HIDDEN.items()]
+
     def tick(i, _):
-        for t in range(STEPS):
-            now, h = during(i, 2 * t + LAG)
+        for name in ORDER:
+            now, h = during(i, AT[name] + LAG)
 
             @pl.when(now)
-            def _(t=t, h=h):
+            def _(name=name, h=h):
                 for r in range(2):
-                    tok_copy(t, h, r).wait_recv()
-
-        for t in range(STEPS):
-            now, h = during(i, 2 * t)
+                    hop_copy(name, h, r).wait_recv()
+                for r in range(2):
+                    hop_copy(name, h, r).wait_send()
+
+        for name in ORDER:
+            now, h = during(i, AT[name])
 
             @pl.when(now)
-            def _(t=t, h=h):
+            def _(name=name, h=h):
+                if name not in TREE:
+                    terms = name.lower() not in TRANSIT
+                    if terms:
+                        term_copy(i).wait_recv()
+                        term_copy(i).wait_send()
+                    add(i % NO, terms, lambda cols: sib[i % NV, :, cols], BELOW[name], h)
                 for r in range(2):
-                    tok_copy(t, h, r).start()
-
-            now, h = during(i, 2 * t + LAG + 1)
-
-            @pl.when(now)
-            def _(t=t, h=h):
-                for r in range(2):
-                    tok_copy(t, h, r).wait_send()
-
-        for name, k in HIDDEN.items():
-            first = 0 if k == 0 else 2 * [s for s, _, _ in DOWN].index(name) + LAG
-            now, h = during(i, first + 2)
+                    hop_copy(name, h, r).start()
+
+        for first, k in swaps:
+            now, h = during(i, first + 1)
 
             @pl.when(now)
             def _(k=k, h=h):
                 swap_copy(k, h).wait_send()
 
-        for name, k in HIDDEN.items():
-            first = 0 if k == 0 else 2 * [s for s, _, _ in DOWN].index(name) + LAG
             now, h = during(i, first)
 
             @pl.when(now)
             def _(k=k, h=h):
                 swap_copy(k, h).start()
 
-        for s, name in enumerate(UP):
-            now, h = during(i, UP0 + 2 * s + LAG)
-
-            @pl.when(now)
-            def _(s=s, h=h):
-                for r in range(2):
-                    out_copy(s, h, r).wait_recv()
-                for r in range(2):
-                    out_copy(s, h, r).wait_send()
-
-        for s, name in enumerate(UP):
-            now, h = during(i, UP0 + 2 * s)
-
-            @pl.when(now)
-            def _(s=s, name=name, h=h):
-                item = 2 * s + h
-                terms = name not in TRANSIT
-                if terms:
-                    term_copy(item).wait_recv()
-                    term_copy(item).wait_send()
-                add(item % NO, terms, lambda cols: sib[item % NV, :, cols], BELOW[name], h)
-                for r in range(2):
-                    out_copy(s, h, r).start()
+        @pl.when(i == AT["H"] + 2)
+        def _():
+            for r in range(2):
+                pl.semaphore_signal(free_sem.at[r], inc=1, device_id={"tp": around[2 * r]}, device_id_type=MESH)
+
+        @pl.when(i == AT["E"] - 1)
+        def _():
+            for r in range(2):
+                pl.semaphore_wait(free_sem.at[r], 1)
 
         now, h = during(i, ROOT0)
 
@@ -244,38 +232,48 @@
         def _(h=h):
             root_copy(h).wait_recv()
             root_copy(h).wait_send()
-            add((ROOT0 - UP0 + h) % NO, True, lambda cols: swp[h, :, cols], ("a", "e"), h)
+            add((ROOT0 + h) % NO, True, lambda cols: swp[h, :, cols], ("A", "E"), h)
             y_store(h).start()
 
-        @pl.when(i == 4)
+        @pl.when(i == 3)
+        def _():
+            for gift in gifts[2::3]:
+                gift.start()
+
+        @pl.when(i == 5)
         def _():
             for h in range(2):
                 x_load(h).wait()
             for load in loads:
                 load.wait()
-            for gift in gifts:
+            for gift in gifts[:2] + gifts[3:5]:
                 gift.wait_recv()
 
-        pair = i // 2
-        firsts = [2 if k == 0 else [s for s, _, _ in DOWN].index(name) + 2 for name, k in HIDDEN.items()]
-        k = table(pair, [firsts.index(p) if p in firsts else -1 for p in range(max(firsts) + 1)] + [-1])
-        k = jnp.where(pair <= max(firsts), k, -1)
+        @pl.when(i == AT["F"] - 1)
+        def _():
+            for gift in gifts[2::3]:
+                gift.wait_recv()
+
+        pair = (i - 1) // 2
+        firsts = [2 if name == "own" else (AT[name] + LAG) // 2 for name in HIDDEN]
+        k = table(pair, [firsts.index(p) if p in firsts else -1 for p in range(max(firsts) + 1)])
+        k = jnp.where((pair >= 0) & (pair <= max(firsts)), k, -1)
 
         @pl.when(k >= 0)
         def _():
             for c in range(8):
-                now, h = during(i, 2 * firsts[c])
+                now, h = during(i, 2 * firsts[c] + 1)
 
                 @pl.when(now)
                 def _(c=c, h=h):
                     swap_copy(c, h).wait_recv()
 
-            compute(k, i % 2)
-
-        item = i + 1 - UP0
-        kinds = [-1 if name in TRANSIT else HIDDEN[name] for name in UP]
-        k = jnp.where((item >= 0) & (item < 2 * STEPS), table(item // 2, kinds), -1)
-        last = i + 1 - ROOT0
+            compute(k, (i - 1) % 2)
+
+        item = i + 1
+        kinds = [HIDDEN.get(name.lower(), -1) if name.isupper() else -1 for name in ORDER]
+        k = jnp.where(item < TICKS, table(item // 2, kinds), -1)
+        last = item - ROOT0
         root = (last >= 0) & (last < 2)
 
         @pl.when((k >= 0) | root)
@@ -332,14 +330,13 @@
                 dma((2,)),
                 dma((2, 3)),
                 dma((2, 3)),
-                dma((2, 2 * STEPS)),
-                dma((2, 2 * STEPS)),
+                dma((2, TICKS)),
+                dma((2, TICKS)),
                 dma((NS,)),
                 dma((NS,)),
-                dma((2, NO)),
-                dma((2, 2 * STEPS)),
                 dma((NV,)),
                 dma((NV,)),
+                pltpu.SemaphoreType.REGULAR((2,)),
             ],
             compiler_params=pltpu.CompilerParams(
                 collective_id=0, has_side_effects=True, vmem_limit_bytes=67_043_328

time: 332 us -> 311 us (0.937)
  Pallas kernels: 328 us -> 308 us
    pallas_call x1, Pallas kernels: 328 us -> 308 us  [step(): pl.pallas_call(functools.partial(kernel, n), out_shape=(jax.ShapeDtypeStr...]
where the time goes in v3:
time: 311 us
  Pallas kernels  308 us (99%)
  local copies, waits for them, and re-layouts  3.13 us (1%)
    pallas_call x1, Pallas kernels, step(): pl.pallas_call(functools.partial(kernel, n), out_shape=(jax.ShapeDtypeStr...  308 us

profile of v3, /device:TPU:97, one launch (start us, length us, event | category | flops | bytes accessed | tf_op | source)
XLA Modules:
  0.0 311.0 jit_solution(14273001103661125830)
XLA Ops:
  0.0 307.9 %shard_map.46 = (bf16[256,4096]{1,0:T(8,128)(2,1)}, bf16[6,128,4096]{2,1,0:T(8,128)(2,1)}) custom-call(bf16[256,4096]{1,0:T(8,128)(2,1)} %x_hbm.1, bf16[4096,512]{1,0:T(8,128)(2,1)} %wg_hbm.1, bf16[4096,512]{1,0:T(8,128)(2,1)} %wu_hbm.1, bf16[512,4096]{1,0:T(8,128)(2,1)} %wd_hbm.1), custom_call_target="tpu_custom_call" | custom-call | tf_op jit(solution)/shard_map/pallas_call | solution.py:309
  307.9 3.1 %copy.6 = bf16[256,4096]{1,0:T(8,128)(2,1)} copy(bf16[256,4096]{1,0:T(8,128)(2,1)} %get-tuple-element.6) | data formatting | bytes 4194304

commit v4 on v0

v4 whole, which is shorter than its diff:
```python
import functools
import math

import jax
import jax.numpy as jnp
from jax import lax
from jax.experimental import pallas as pl
from jax.experimental.pallas import tpu as pltpu
from jax.sharding import PartitionSpec as P

MESH = pl.DeviceIdType.MESH
ROLES = 7
SEQ = ((3, 1), (5, 0), (4, 0), (4, 1), (2, 1), (6, 0), (3, 0), (5, 1), (2, 0), (6, 1), (1, 1), (7, 0), (1, 0), (7, 1), (0, 0), (0, 1))
TICK = (22, 23, 24, 25, 26, 27, 28, 29, 30, 31, 32, 33, 34, 35, 37, 38)
TICK0, TICKS = TICK[0], TICK[-1] + 1
PASS = (('w', 1, 27), ('v', 0, 28), ('w', 0, 33), ('v', 1, 34))
SLOT = {name: 2 * k for k, name in enumerate((4, 2, 6, 1, 7, "w", "v"))}
BELOW = {(3, 0): (4,), (5, 1): (4,)}
BELOW |= {(role, h): below for role, below in ((1, (2, "w")), (7, (6, "v")), (0, (1, 7))) for h in range(2)}
HOP = {(4, 0): "b", (4, 1): "f"} | {
    (role, h): hop for role, hop in ((3, "kb"), (5, "kf"), (2, "b"), (6, "f"), (1, "b"), (7, "f")) for h in range(2)
}
EARLY = 8
JOBS = (0, 0, 1, 1, 1, 1, 1, 0, 1, 0, 1, 0, 1, 0, 2, 2, 2, 2, 2, 2, 2, 2, 1, 1, 1, 1, 1, 1, 1, 1)
WAIT = 14
NO, NV = 5, 2


def table(index, values):
    result = values[0]
    for k, value in enumerate(values[1:], 1):
        result = jnp.where(index == k, value, result)
    return result


def kernel(
    n, x_hbm, wg_hbm, wu_hbm, wd_hbm, y_hbm, far, swp, via,
    blk, arr, out, term, sib, acc, hid, wg, wu, wd,
    w_sem, y_sem, blk_sem, w_send, w_recv, tok_send, tok_recv, swap_send, swap_recv,
    sum_send, sum_recv, via_send, via_recv, term_send, term_recv,
):
    half = x_hbm.shape[0] // 2
    depth, width = x_hbm.shape[1], wg_hbm.shape[1]
    part = width // 2
    side = math.isqrt(n // 2)
    me = lax.axis_index("tp")
    chip, core = me // 2, me % 2
    gx, gy = chip // side, chip % side
    odd = (gx + gy) % 2
    sibling = chip * 2 + 1 - core

    def device(dx, dy):
        return (((gx + dx + side) % side) * side + (gy + dy + side) % side) * 2 + core

    ring = device(1 - odd, -odd), device(-odd, 1 - odd)
    cross = device(odd - 1, odd), device(odd, odd - 1)
    around = {
        "f": jnp.where(core == 0, ring[0], ring[1]),
        "b": jnp.where(core == 0, ring[1], ring[0]),
        "kb": jnp.where(core == 0, cross[0], cross[1]),
        "kf": jnp.where(core == 0, cross[1], cross[0]),
    }

    def remote(src, dst, send, recv, target):
        return pltpu.make_async_remote_copy(
            src_ref=src, dst_ref=dst, send_sem=send, recv_sem=recv, device_id={"tp": target}, device_id_type=MESH
        )

    def own(h):
        return x_hbm.at[pl.ds(h * half, half)]

    def tok_copy(j, own_half=None):
        src = own(own_half) if own_half is not None else far.at[j - 2]
        return remote(src, far.at[j], tok_send.at[j], tok_recv.at[j], around["f"])

    def swap_copy(c, own_half=None):
        src = own(own_half) if own_half is not None else far.at[c - 2]
        return remote(src, swp.at[c], swap_send.at[c], swap_recv.at[c], sibling)

    def sum_copy(k):
        role, h = SEQ[k]
        if role in (3, 5):
            return remote(
                out.at[k % NO], via.at[role - 3 + h], sum_send.at[k], via_recv.at[role - 3 + h], around[HOP[role, h]]
            )
        return remote(
            out.at[k % NO], arr.at[SLOT[role] + h], sum_send.at[k], sum_recv.at[SLOT[role] + h], around[HOP[role, h]]
        )

    def via_in(kind, h):
        return sum_copy(SEQ.index((3 if kind == "w" else 5, h)))

    def via_copy(kind, h):
        here = (0 if kind == "w" else 2) + h
        return remote(
            via.at[here], arr.at[SLOT[kind] + h], via_send.at[here], sum_recv.at[SLOT[kind] + h],
            around["kb" if kind == "w" else "kf"],
        )

    def arrival(name, h):
        if name in ("w", "v"):
            return via_copy(name, h)
        return sum_copy(SEQ.index((name, h)))

    def term_copy(k):
        return remote(term.at[k % NV], sib.at[k % NV], term_send.at[k % NV], term_recv.at[k % NV], sibling)

    def job_block(z):
        return jnp.where(z < EARLY, z, jnp.where(z < 2 * EARLY, z - EARLY, z // 2))

    def blk_copies(z, src):
        slot = z % 2
        return (
            pltpu.make_async_copy(src, blk.at[slot, pl.ds(0, half)], blk_sem.at[slot, 0]),
            pltpu.make_async_copy(swp.at[job_block(z)], blk.at[slot, pl.ds(half, half)], blk_sem.at[slot, 1]),
        )

    def blk_load(z):
        c = job_block(z)

        @pl.when(c < 2)
        def _():
            for load in blk_copies(z, own(c)):
                load.start()

        @pl.when(c >= 2)
        def _():
            for load in blk_copies(z, far.at[c - 2]):
                load.start()

    def y_store(h):
        k = SEQ.index((0, h))
        return pltpu.make_async_copy(out.at[k % NO], y_hbm.at[pl.ds(h * half, half)], y_sem.at[h])

    loads, gifts = [], []
    for g in range(2):
        cols = pl.ds(g * part, part)
        for k, (a, b) in enumerate(((wg_hbm, wg), (wu_hbm, wu))):
            loads.append(pltpu.make_async_copy(a.at[:, cols], b.at[g], w_sem.at[2 * k + g]))
            gifts.append(
                remote(a.at[:, cols], b.at[2 + g], w_send.at[2 * k + g], w_recv.at[2 * k + g], around["kb"])
            )
    loads.append(pltpu.make_async_copy(wd_hbm, wd.at[pl.ds(0, width)], w_sem.at[4]))
    gifts.append(remote(wd_hbm, wd.at[pl.ds(width, width)], w_send.at[4], w_recv.at[4], around["kb"]))

    barrier = pltpu.get_barrier_semaphore()
    for target in (*around.values(), sibling):
        pl.semaphore_signal(barrier, inc=1, device_id={"tp": target}, device_id_type=MESH)
    pl.semaphore_wait(barrier, 5)
    for h in range(2):
        tok_copy(h, h).start()
    for gift in gifts:
        gift.start()
    for h in range(2):
        swap_copy(h, h).start()
    for load in loads:
        load.start()

    def compute(z):
        c, late = job_block(z), jnp.where(z < EARLY, 0, jnp.where(z < 2 * EARLY, 1, z % 2))
        for g in range(2):
            block = blk[z % 2]
            group = 2 * late + g
            gate = jnp.dot(block, wg[group], preferred_element_type=jnp.float32)
            up = jnp.dot(block, wu[group], preferred_element_type=jnp.float32)
            cols = pl.ds(pl.multiple_of(group * part, part), part)
            hid[c, :, cols] = (jax.nn.silu(gate) * up).astype(jnp.bfloat16)

    def project(item, slot):
        step = min(512, depth)
        for c in range(0, depth, step):
            t = jnp.dot(hid[item], wd[:, c : c + step], preferred_element_type=jnp.float32)
            acc[:, c : c + step] = t[:half]
            term[slot, :, c : c + step] = t[half:].astype(jnp.bfloat16)

    def add(k):
        role, h = SEQ[k]
        step = min(512, depth)

        def piece(c, _):
            cols = pl.ds(pl.multiple_of(c * step, step), step)
            total = acc[:, cols] + sib[k % NV, :, cols].astype(jnp.float32)
            for name in BELOW.get((role, h), ()):
                total = total + arr[SLOT[name] + h, :, cols].astype(jnp.float32)
            out[k % NO, :, cols] = total.astype(jnp.bfloat16)
            return 0

        lax.fori_loop(0, depth // step, piece, 0)

    blocks = 2 * ROLES

    def tick(i, _):
        j = i // 2
        due = i % 2 == 0

        @pl.when(due & (j < blocks))
        def _():
            tok_copy(j, 0).wait_recv()

        @pl.when(due & (j < blocks - 2))
        def _():
            tok_copy(j + 2).start()

        @pl.when(due & (j < blocks))
        def _():
            swap_copy(j + 2).start()

        for kind, h, when in PASS:

            @pl.when(i == when)
            def _(kind=kind, h=h):
                via_in(kind, h).wait_recv()
                via_copy(kind, h).start()

        for k, (role, h) in enumerate(SEQ):

            @pl.when(i == TICK[k])
            def _(k=k, role=role, h=h):
                for name in BELOW.get((role, h), ()):
                    arrival(name, h).wait_recv()
                if k >= NO:
                    sum_copy(k - NO).wait_send()
                term_copy(k).wait_recv()
                term_copy(k).wait_send()
                add(k)
                if role:
                    sum_copy(k).start()
                else:
                    y_store(h).start()

        @pl.when(i == [k for k, count in enumerate(JOBS) if count][0])
        def _():
            for load in loads:
                load.wait()

        @pl.when(i == WAIT)
        def _():
            for gift in gifts[:-1]:
                gift.wait_recv()

        first = table(i, [sum(JOBS[:k]) for k in range(len(JOBS))])
        count = jnp.where(i < len(JOBS), table(i, JOBS), 0)

        def job(z, _):
            @pl.when(z < EARLY)
            def _():
                swap_copy(z, 0).wait_recv()
                blk_load(z)

            for load in blk_copies(z, own(0)):
                load.wait()

            @pl.when((z + 1 >= 2 * EARLY) & (z + 1 < 2 * (blocks + 2)) & (z % 2 == 1))
            def _():
                swap_copy(job_block(z + 1), 0).wait_recv()

            @pl.when((z + 1 >= EARLY) & (z + 1 < 2 * (blocks + 2)))
            def _():
                blk_load(z + 1)

            compute(z)
            return 0

        lax.fori_loop(first, first + count, job, 0)

        @pl.when(i == TICK0 - 1)
        def _():
            gifts[-1].wait_recv()

        places = {t - 1: k for k, t in enumerate(TICK)}
        k = jnp.where(i >= TICK0 - 1, table(i - TICK0 + 1, [places.get(t, -1) for t in range(TICK0 - 1, TICKS)]), -1)

        @pl.when(k >= 0)
        def _():
            project(table(k, [2 * role + h for role, h in SEQ]), k % NV)
            term_copy(k).start()

        return 0

    lax.fori_loop(0, TICKS, tick, 0)
    for gift in gifts:
        gift.wait_send()
    for j in range(2):
        tok_copy(j, j).wait_send()
        swap_copy(j, j).wait_send()
    for j in range(2, blocks):
        tok_copy(j).wait_send()
    for c in range(2, blocks + 2):
        swap_copy(c).wait_send()
    for k, (role, _) in enumerate(SEQ):
        if role and k >= len(SEQ) - NO:
            sum_copy(k).wait_send()
    for kind, h, _ in PASS:
        via_copy(kind, h).wait_send()
    for h in range(2):
        y_store(h).wait()


def solution(mesh):
    n = mesh.shape["tp"]

    def step(x, w_gate, w_up, w_down):
        rows, depth = x.shape
        width = w_gate.shape[1]
        half, part = rows // 2, width // 2
        vmem, dma = pltpu.VMEM, pltpu.SemaphoreType.DMA
        blocks = 2 * ROLES
        out = pl.pallas_call(
            functools.partial(kernel, n),
            out_shape=(
                jax.ShapeDtypeStruct((rows, depth), jnp.bfloat16),
                jax.ShapeDtypeStruct((blocks, half, depth), jnp.bfloat16),
                jax.ShapeDtypeStruct((blocks + 2, half, depth), jnp.bfloat16),
                jax.ShapeDtypeStruct((4, half, depth), jnp.bfloat16),
            ),
            in_specs=[pl.BlockSpec(memory_space=pl.ANY)] * 4,
            out_specs=(pl.BlockSpec(memory_space=pl.ANY),) * 4,
            scratch_shapes=[
                vmem((2, 2 * half, depth), jnp.bfloat16),
                vmem((2 * len(SLOT), half, depth), jnp.bfloat16),
                vmem((NO, half, depth), jnp.bfloat16),
                vmem((NV, half, depth), jnp.bfloat16),
                vmem((NV, half, depth), jnp.bfloat16),
                vmem((half, depth), jnp.float32),
                vmem((blocks + 2, 2 * half, 2 * width), jnp.bfloat16),
                vmem((4, depth, part), jnp.bfloat16),
                vmem((4, depth, part), jnp.bfloat16),
                vmem((2 * width, depth), jnp.bfloat16),
                dma((5,)),
                dma((2,)),
                dma((2, 2)),
                dma((5,)),
                dma((5,)),
                dma((blocks,)),
                dma((blocks,)),
                dma((blocks + 2,)),
                dma((blocks + 2,)),
                dma((len(SEQ),)),
                dma((2 * len(SLOT),)),
                dma((4,)),
                dma((4,)),
                dma((NV,)),
                dma((NV,)),
            ],
            compiler_params=pltpu.CompilerParams(
                collective_id=0, has_side_effects=True, vmem_limit_bytes=67_043_328
            ),
        )(x, w_gate, w_up, w_down)
        return out[0]

    return jax.shard_map(
        step,
        mesh=mesh,
        in_specs=(P(("dp", "tp"), None), P(None, "tp"), P(None, "tp"), P("tp", None)),
        out_specs=P(("dp", "tp"), None),
        check_vma=False,
    )
```

time: 623 us -> 286 us (0.46)
  waiting for transfers between devices: 486 us -> 0 us
  Pallas kernels: 0 us -> 282 us
  matrix products: 124 us -> 0 us
  between operations: 13.4 us -> 0.01 us
    unnamed x3 -> x0, waiting for transfers between devices: 284 us -> none
    pallas_call x0 -> x1, Pallas kernels: none -> 282 us  [step(): pl.pallas_call(functools.partial(kernel, n), out_shape=(jax.ShapeDtypeStr...]
    all_gather x1 -> x0, waiting for transfers between devices: 202 us -> none  [step(): rows = lax.all_gather(x, 'tp', axis=0, tiled=True)]
    dot_general x2 -> x0, matrix products: 124 us -> none  [the longest x1 81 us: step(): jnp.dot(hidden, w_down, preferred_element_type=jnp.float32)]
  transfers between devices with their start and end apart: 2 -> 0, of which waited for: 2 -> 0; matrix products, arithmetic and copies ran while one was open for 0% -> 0% of each run, Pallas kernels for 0% -> 0%
where the time goes in v4:
time: 286 us
  Pallas kernels  282 us (99%)
  local copies, waits for them, and re-layouts  3.13 us (1%)
    pallas_call x1, Pallas kernels, step(): pl.pallas_call(functools.partial(kernel, n), out_shape=(jax.ShapeDtypeStr...  282 us

profile of v4, /device:TPU:97, one launch (start us, length us, event | category | flops | bytes accessed | tf_op | source)
XLA Modules:
  0.0 285.6 jit_solution(9100209207416658966)
XLA Ops:
  0.0 282.5 %shard_map.46 = (bf16[256,4096]{1,0:T(8,128)(2,1)}, bf16[14,128,4096]{2,1,0:T(8,128)(2,1)}, bf16[16,128,4096]{2,1,0:T(8,128)(2,1)}, bf16[4,128,4096]{2,1,0:T(8,128)(2,1)}) custom-call(bf16[256,4096]{1,0:T(8,128)(2,1)} %x_hbm.1, bf16[4096,512]{1,0:T(8,128)(2,1)} %wg_hbm.1, bf16[4096,512]{1,0:T(8,128)(2,1)} %wu_hbm.1, bf16[512,4096]{1,0:T(8,128)(2,1)} %wd_hbm.1), custom_call_target="tpu_custom_call" | custom-call | tf_op jit(solution)/shard_map/pallas_call | solution.py:308
  282.5 3.1 %copy.6 = bf16[256,4096]{1,0:T(8,128)(2,1)} copy(bf16[256,4096]{1,0:T(8,128)(2,1)} %get-tuple-element.6) | data formatting | bytes 4194304

commit v5 on v4

--- a/solution.py
+++ b/solution.py
@@ -143,6 +143,8 @@
     loads.append(pltpu.make_async_copy(wd_hbm, wd.at[pl.ds(0, width)], w_sem.at[4]))
     gifts.append(remote(wd_hbm, wd.at[pl.ds(width, width)], w_send.at[4], w_recv.at[4], around["kb"]))
 
+    for load in loads:
+        load.start()
     barrier = pltpu.get_barrier_semaphore()
     for target in (*around.values(), sibling):
         pl.semaphore_signal(barrier, inc=1, device_id={"tp": target}, device_id_type=MESH)
@@ -153,8 +155,6 @@
         gift.start()
     for h in range(2):
         swap_copy(h, h).start()
-    for load in loads:
-        load.start()
 
     def compute(z):
         c, late = job_block(z), jnp.where(z < EARLY, 0, jnp.where(z < 2 * EARLY, 1, z % 2))

time: 286 us -> 286 us (level)
  no operation moved by 1% of the time
where the time goes in v5:
time: 286 us
  Pallas kernels  282 us (99%)
  local copies, waits for them, and re-layouts  3.13 us (1%)
    pallas_call x1, Pallas kernels, step(): pl.pallas_call(functools.partial(kernel, n), out_shape=(jax.ShapeDtypeStr...  282 us

profile of v5, /device:TPU:97, one launch (start us, length us, event | category | flops | bytes accessed | tf_op | source)
XLA Modules:
  0.0 285.6 jit_solution(67954228418398545)
XLA Ops:
  0.0 282.5 %shard_map.46 = (bf16[256,4096]{1,0:T(8,128)(2,1)}, bf16[14,128,4096]{2,1,0:T(8,128)(2,1)}, bf16[16,128,4096]{2,1,0:T(8,128)(2,1)}, bf16[4,128,4096]{2,1,0:T(8,128)(2,1)}) custom-call(bf16[256,4096]{1,0:T(8,128)(2,1)} %x_hbm.1, bf16[4096,512]{1,0:T(8,128)(2,1)} %wg_hbm.1, bf16[4096,512]{1,0:T(8,128)(2,1)} %wu_hbm.1, bf16[512,4096]{1,0:T(8,128)(2,1)} %wd_hbm.1), custom_call_target="tpu_custom_call" | custom-call | tf_op jit(solution)/shard_map/pallas_call | solution.py:308
  282.5 3.1 %copy.6 = bf16[256,4096]{1,0:T(8,128)(2,1)} copy(bf16[256,4096]{1,0:T(8,128)(2,1)} %get-tuple-element.6) | data formatting | bytes 4194304
